TPU v7x, 256 devices: a whole 4x4x8 slice. The times are simulated.
256 devices in a mesh: dp: 128 (over x, z, y_hi, core), outer: 2 (over y_lo).
Axes of the slice: x: 4, y: 4 (y_hi: 2, y_lo: 2; y = y_hi * 2 + y_lo), z: 8, core: 2. Of those that a mesh axis runs over, the one named last changes fastest.
Arguments:
- images: bfloat16 [16384, 1024], P('dp'), may hold values from -8 to 8
- texts: bfloat16 [16384, 1024], P(('dp', 'outer')), may hold values from -8 to 8
- logit_scale: float32 [1], replicated, may hold values from 70 to 100
Outputs:
- image_loss: float32 [16384], P(('dp', 'outer'))
- text_loss: float32 [16384], P(('dp', 'outer'))
All inputs are finite; a program needn't handle non-finite values.
Results may differ from a plain program's by a relative error of at most 0.003.
Values may be sent and summed in bfloat16 or wider, within the bound.
No kernel may reach another device: no remote copies, remote signals or barrier semaphores. Data moves between devices by JAX's collectives and lax.ppermute only.
A program may use at most 64 MiB of HBM per device.

v0:
```python
import jax
import jax.numpy as jnp
from jax import lax
from jax.sharding import PartitionSpec as P


def side_by_side(arrays, axis, split_dim, concat_dim, along):
    ends, at = ([], 0)
    for a in arrays[:-1]:
        at += a.shape[along]
        ends.append(at)
    both = jnp.concatenate(arrays, axis=along)
    return tuple(
        jnp.split(
            lax.all_to_all(both, axis, split_axis=split_dim, concat_axis=concat_dim, tiled=True),
            ends,
            axis=along,
        )
    )


def partner(block, axis, apart):
    count = lax.axis_size(axis)
    route = []
    for low in range(count):
        high = low | 1 << apart
        if high != low and high < count:
            route += [(low, high), (high, low)]
    return lax.ppermute(block, axis, route)


def normalise(features):
    widened = features.astype(jnp.float32)
    return (widened * lax.rsqrt(jnp.sum(widened * widened, axis=1, keepdims=True) + 1.0)).astype(
        jnp.bfloat16
    )


def merge_states(first, second):
    peak = jnp.maximum(first[0], second[0])
    return (peak, first[1] * jnp.exp(first[0] - peak) + second[1] * jnp.exp(second[0] - peak))


def on_device(images, texts, logit_scale):
    image_unit = normalise(images)
    text_unit = normalise(texts)
    factor = logit_scale[0]
    img_rows = image_unit.shape[0]
    txt_rows = text_unit.shape[0]
    cycle_size = lax.axis_size("dp")
    row_peak = jnp.full((img_rows,), -1e30, jnp.float32)
    scores = (
        jnp.einsum(
            "id,jd->ij",
            image_unit,
            lax.all_gather(text_unit, "dp", axis=0, tiled=True),
            preferred_element_type=jnp.float32,
        )
        * factor
    )
    block_peak = jnp.max(scores, axis=0)
    block_total = jnp.sum(jnp.exp(scores - block_peak), axis=0)
    col_peak = block_peak
    col_total = block_total
    new_peak = jnp.maximum(row_peak, jnp.max(scores, axis=1))
    row_total = jnp.sum(jnp.exp(scores - new_peak[:, None]), axis=1)
    row_peak, row_total, col_peak, col_total = (new_peak, row_total, col_peak, col_total)
    peak_table, total_table = side_by_side(
        (col_peak.reshape(cycle_size, txt_rows), col_total.reshape(cycle_size, txt_rows)),
        "dp",
        0,
        0,
        1,
    )
    text_peak = jnp.max(peak_table, axis=0)
    text_total = jnp.sum(total_table * jnp.exp(peak_table - text_peak), axis=0)
    text_lse = text_peak + jnp.log(text_total)
    outer_index = lax.axis_index("outer")
    group_count = img_rows // txt_rows
    peak_halves = row_peak.reshape(group_count, txt_rows)
    total_halves = row_total.reshape(group_count, txt_rows)
    own_half = (
        lax.dynamic_index_in_dim(peak_halves, outer_index, 0, keepdims=False),
        lax.dynamic_index_in_dim(total_halves, outer_index, 0, keepdims=False),
    )
    partner_half = (
        lax.dynamic_index_in_dim(peak_halves, 1 - outer_index, 0, keepdims=False),
        lax.dynamic_index_in_dim(total_halves, 1 - outer_index, 0, keepdims=False),
    )
    received = partner((partner_half[0], partner_half[1]), "outer", 0)
    image_peak, image_total = merge_states(own_half, received)
    image_own = lax.dynamic_slice_in_dim(image_unit, outer_index * txt_rows, txt_rows, 0)
    diagonal = (
        jnp.sum(image_own.astype(jnp.float32) * text_unit.astype(jnp.float32), axis=1) * factor
    )
    return (image_peak + jnp.log(image_total) - diagonal, text_lse - diagonal)


def solution(mesh):
    in_specs = (P("dp", None), P(("dp", "outer"), None), P())
    out_specs = (P(("dp", "outer")), P(("dp", "outer")))
    return jax.shard_map(
        on_device, mesh=mesh, in_specs=in_specs, out_specs=out_specs, check_vma=False
    )
```

profile of v0, /device:TPU:1, one launch (start us, length us, event | category | flops | bytes accessed | tf_op | source)
XLA Modules:
  0.0 210.6 jit_solution(15811068224282388094)
XLA Ops:
  7.2 0.0 all-gather.2.cloned.1.call-start
  7.2 1.1 fusion
  8.3 1.1 fusion.1
  9.4 1.0 fusion.2
  10.4 1.8 multiply_reduce_fusion
  12.2 0.0 all-gather.2.cloned.1.call-update
  12.9 151.6 %all-gather.2.cloned.1.call-done = bf16[8192,1024]{1,0:T(8,128)(2,1)} async-done(((bf16[64,1024]{1,0:T(8,128)(2,1)}), bf16[8192,1024]{1,0:T(8,128)(2,1)}) %all-gather.2.cloned.1.call-update) | async-done | bytes 16777232 | tf_op jit(solution)/shard_map/all_gather | solution.py:56
  164.5 13.3 %fusion.12 = (f32[8192]{0:T(1024)S(1)}, f32[128]{0:T(128)S(1)}, f32[128,8192]{1,0:T(8,128)}) fusion(f32[]{:T(128)} %bitcast.23, bf16[128,1024]{1,0:T(8,128)(2,1)S(1)} %fusion.1, bf16[8192,1024]{1,0:T(8,128)(2,1)} %all-gather.2.cloned.1.call-done), kind=kOutput, calls=%fused_computation.33 | convolution fusion | flops 2150621184 | bytes 21266948 | tf_op jit(solution)/shard_map/id,jd->ij/dot_general | solution.py:53
  177.8 0.1 reshape.37
  177.9 3.5 %exponential_reduce_fusion = (f32[8192]{0:T(1024)S(1)}, f32[128]{0:T(128)S(1)}) fusion(f32[128,8192]{1,0:T(8,128)} %get-tuple-element.10, f32[8192]{0:T(1024)S(1)} %get-tuple-element.4, f32[128]{0:T(128)S(1)} %broadcast_maximum_fusion), kind=kLoop, calls=%fused_computation.1 | loop fusion | flops 4185984 | bytes 4260864 | tf_op jit(solution)/shard_map/reduce_sum | solution.py:62
  181.4 0.1 reshape.38
  181.5 0.7 pad_maximum_fusion
  182.2 8.8 %all-to-all-start = ((f32[128,1,128]{2,1,0:T(1,128)}), f32[128,1,128]{2,1,0:T(1,128)S(1)}, u32[]{:S(2)}, u32[]{:S(2)}) async-start(f32[128,1,128]{2,1,0:T(1,128)} %bitcast.6), calls=%async_computation | async-start | bytes 131072 | tf_op jit(solution)/shard_map/all_to_all | solution.py:15
  191.0 0.1 reshape.36
  191.1 0.1 max_broadcast_in_dim.12
  191.1 1.2 collective-permute-start.1
  192.3 0.3 collective-permute-start
  192.6 10.4 %all-to-all-done = f32[128,1,128]{2,1,0:T(1,128)S(1)} async-done(((f32[128,1,128]{2,1,0:T(1,128)}), f32[128,1,128]{2,1,0:T(1,128)S(1)}, u32[]{:S(2)}, u32[]{:S(2)}) %all-to-all-start) | async-done | bytes 65568 | tf_op jit(solution)/shard_map/all_to_all | solution.py:15
  203.1 0.1 fusion.4
  203.2 0.0 collective-permute-done.1
  203.2 0.0 collective-permute-done
  203.2 0.5 add_subtract_fusion
  (6 shorter events, 0.1 us)
Async XLA Ops:
  7.2 157.3 %all-gather.2.cloned.1.call-start = ((), (), s32[]{:S(2)}) async-start(), calls=%async_computation.1 | async-start | bytes 16908288 | tf_op jit(solution)/shard_map/all_gather | solution.py:56
  182.2 20.9 %all-to-all-start = ((f32[128,1,128]{2,1,0:T(1,128)}), f32[128,1,128]{2,1,0:T(1,128)S(1)}, u32[]{:S(2)}, u32[]{:S(2)}) async-start(f32[128,1,128]{2,1,0:T(1,128)} %bitcast.6), calls=%async_computation | async-start | bytes 131072 | tf_op jit(solution)/shard_map/all_to_all | solution.py:15
  191.1 12.1 %collective-permute-start.1 = (f32[64]{0:T(128)S(1)}, f32[64]{0:T(128)S(1)}, u32[]{:S(2)}, u32[]{:S(2)}) collective-permute-start(f32[64]{0:T(128)S(1)} %fusion.10), channel_id=1, source_target_pairs={{0,1},{1,0},{2,3},{3,2},{4,5},{5,4},{6,7},{7,6},{8,9},{9,8},{10,11... | collective-permute-start | bytes 776 | tf_op jit(solution)/shard_map/ppermute | solution.py:29
  192.3 10.9 %collective-permute-start = (f32[64]{0:T(128)S(1)}, f32[64]{0:T(128)S(1)}, u32[]{:S(2)}, u32[]{:S(2)}) collective-permute-start(f32[64]{0:T(128)S(1)} %fusion.6), channel_id=1, source_target_pairs={{0,1},{1,0},{2,3},{3,2},{4,5},{5,4},{6,7},{7,6},{8,9},{9,8},{10,11... | collective-permute-start | bytes 776 | tf_op jit(solution)/shard_map/ppermute | solution.py:29
Sparse Core Ops, SparseCore 0:
  12.3 152.1 all-gather.1
where the time goes:
time: 211 us
  waiting for transfers between devices  162 us (77%)
  between operations  14.7 us (7%)
  matrix products  13.3 us (6%)
  starting transfers between devices  10.3 us (5%)
  other arithmetic  9.85 us (5%)
    all_gather x1, waiting for transfers between devices, on_device(): lax.all_gather(text_unit, 'dp', axis=0, tiled=True)  152 us
    dot_general x1, matrix products, on_device(): jnp.einsum('id,jd->ij', image_unit, lax.all_gather(text_unit, 'dp', axis=...  13.3 us
    all_to_all x1, waiting for transfers between devices, side_by_side(): lax.all_to_all(both, axis, split_axis=split_dim, concat_axis=concat_dim,...  10.4 us
    all_to_all x1, starting transfers between devices, side_by_side(): lax.all_to_all(both, axis, split_axis=split_dim, concat_axis=concat_dim,...  8.76 us
  transfers between devices with their start and end apart: 4, of which 2 were waited for; matrix products, arithmetic and copies ran while one was open for 0% of the time, Pallas kernels for 0%

commit v1 on v0

--- a/solution.py
+++ b/solution.py
@@ -2,6 +2,11 @@
 import jax.numpy as jnp
 from jax import lax
 from jax.sharding import PartitionSpec as P
+
+
+def swapped_in(x, name, dim):
+    outgoing = jnp.stack([x] * lax.axis_size(name))
+    return jnp.concatenate(lax.all_to_all(outgoing, name, 0, 0), axis=dim)
 
 
 def side_by_side(arrays, axis, split_dim, concat_dim, along):
@@ -53,7 +58,7 @@
         jnp.einsum(
             "id,jd->ij",
             image_unit,
-            lax.all_gather(text_unit, "dp", axis=0, tiled=True),
+            swapped_in(text_unit, "dp", 0),
             preferred_element_type=jnp.float32,
         )
         * factor

time: 211 us -> 434 us (2.06)
  waiting for transfers between devices: 162 us -> 375 us
  starting transfers between devices: 10.3 us -> 29.2 us
  between operations: 14.7 us -> 1.34 us
  local copies, waits for them, and re-layouts: 0.32 us -> 6.36 us
    all_to_all x0 -> x1, waiting for transfers between devices: none -> 364 us  [swapped_in(): return jnp.concatenate(lax.all_to_all(outgoing, name, 0, 0), axis=dim)]
    all_gather x1 -> x0, waiting for transfers between devices: 152 us -> none  [on_device(): lax.all_gather(text_unit, 'dp', axis=0, tiled=True)]
    all_to_all x0 -> x1, starting transfers between devices: none -> 16.8 us  [swapped_in(): return jnp.concatenate(lax.all_to_all(outgoing, name, 0, 0), axis=dim)]
    another operation x0 -> x1, local copies, waits for them, and re-layouts: none -> 6.04 us  [swapped_in(): outgoing = jnp.stack([x] * lax.axis_size(name))]
where the time goes in v1:
time: 434 us
  waiting for transfers between devices  375 us (86%)
  starting transfers between devices  29.2 us (7%)
  matrix products  13.3 us (3%)
  other arithmetic  9.21 us (2%)
  local copies, waits for them, and re-layouts  6.36 us (1%)
    all_to_all x1, waiting for transfers between devices, swapped_in(): return jnp.concatenate(lax.all_to_all(outgoing, name, 0, 0), axis=dim)  364 us
    all_to_all x1, starting transfers between devices, swapped_in(): return jnp.concatenate(lax.all_to_all(outgoing, name, 0, 0), axis=dim)  16.8 us
    dot_general x1, matrix products, on_device(): jnp.einsum('id,jd->ij', image_unit, swapped_in(text_unit, 'dp', 0), prefe...  13.3 us
    all_to_all x1, starting transfers between devices, side_by_side(): lax.all_to_all(both, axis, split_axis=split_dim, concat_axis=concat_dim,...  10.9 us
    all_to_all x1, waiting for transfers between devices, side_by_side(): lax.all_to_all(both, axis, split_axis=split_dim, concat_axis=concat_dim,...  10.4 us
  transfers between devices with their start and end apart: 4, of which 2 were waited for; matrix products, arithmetic and copies ran while one was open for 0% of the time, Pallas kernels for 0%

profile of v1, /device:TPU:1, one launch (start us, length us, event | category | flops | bytes accessed | tf_op | source)
XLA Modules:
  0.0 434.1 jit_solution(14180775593307750168)
XLA Ops:
  0.6 1.1 fusion
  1.7 1.1 fusion.1
  2.8 1.0 fusion.2
  3.8 1.1 multiply_reduce_fusion
  5.0 6.0 %stack.2 = bf16[128,64,1024]{2,1,0:T(8,128)(2,1)} broadcast(bf16[64,1024]{1,0:T(8,128)(2,1)S(1)} %get-tuple-element.7), dimensions={1,2} | broadcast | bytes 16908288 | tf_op jit(solution)/shard_map/stack | solution.py:8
  11.0 16.8 %all-to-all-start = ((bf16[128,64,1024]{2,1,0:T(8,128)(2,1)}), bf16[128,64,1024]{2,1,0:T(8,128)(2,1)}, u32[]{:S(2)}, u32[]{:S(2)}) async-start(bf16[128,64,1024]{2,1,0:T(8,128)(2,1)} %stack.2), calls=%async_computation | async-start | bytes 33554432 | tf_op jit(solution)/shard_map/all_to_all | solution.py:9
  28.5 364.2 %all-to-all-done = bf16[128,64,1024]{2,1,0:T(8,128)(2,1)} async-done(((bf16[128,64,1024]{2,1,0:T(8,128)(2,1)}), bf16[128,64,1024]{2,1,0:T(8,128)(2,1)}, u32[]{:S(2)}, u32[]{:S(2)}) %all-to-all-start) | async-done | bytes 16777248 | tf_op jit(solution)/shard_map/all_to_all | solution.py:9
  392.8 13.3 %fusion.12 = (f32[8192]{0:T(1024)S(1)}, f32[128]{0:T(128)S(1)}, f32[128,8192]{1,0:T(8,128)}) fusion(f32[]{:T(128)} %bitcast.24, bf16[128,1024]{1,0:T(8,128)(2,1)S(1)} %fusion.1, bf16[8192,1024]{1,0:T(8,128)(2,1)} %bitcast), kind=kOutput, calls=%fused_computation.33 | convolution fusion | flops 2150621184 | bytes 21266948 | tf_op jit(solution)/shard_map/id,jd->ij/dot_general | solution.py:58
  406.1 0.1 reshape.43
  406.2 3.5 exponential_reduce_fusion
  409.7 0.1 reshape.44
  409.7 0.7 pad_maximum_fusion
  410.4 10.9 %all-to-all-start.1 = ((f32[128,1,128]{2,1,0:T(1,128)}), f32[128,1,128]{2,1,0:T(1,128)S(1)}, u32[]{:S(2)}, u32[]{:S(2)}) async-start(f32[128,1,128]{2,1,0:T(1,128)} %bitcast.7), calls=%async_computation.1 | async-start | bytes 131072 | tf_op jit(solution)/shard_map/all_to_all | solution.py:20
  421.3 0.1 reshape.42
  421.4 0.1 max_broadcast_in_dim.12
  421.5 0.4 collective-permute-start.1
  421.9 1.1 collective-permute-start
  423.0 10.4 %all-to-all-done.1 = f32[128,1,128]{2,1,0:T(1,128)S(1)} async-done(((f32[128,1,128]{2,1,0:T(1,128)}), f32[128,1,128]{2,1,0:T(1,128)S(1)}, u32[]{:S(2)}, u32[]{:S(2)}) %all-to-all-start.1) | async-done | bytes 65568 | tf_op jit(solution)/shard_map/all_to_all | solution.py:20
  433.5 0.1 fusion.4
  433.6 0.0 collective-permute-done.1
  433.6 0.0 collective-permute-done
  433.6 0.5 add_subtract_fusion
  (6 shorter events, 0.1 us)
Async XLA Ops:
  11.0 381.7 %all-to-all-start = ((bf16[128,64,1024]{2,1,0:T(8,128)(2,1)}), bf16[128,64,1024]{2,1,0:T(8,128)(2,1)}, u32[]{:S(2)}, u32[]{:S(2)}) async-start(bf16[128,64,1024]{2,1,0:T(8,128)(2,1)} %stack.2), calls=%async_computation | async-start | bytes 33554432 | tf_op jit(solution)/shard_map/all_to_all | solution.py:9
  410.4 23.0 %all-to-all-start.1 = ((f32[128,1,128]{2,1,0:T(1,128)}), f32[128,1,128]{2,1,0:T(1,128)S(1)}, u32[]{:S(2)}, u32[]{:S(2)}) async-start(f32[128,1,128]{2,1,0:T(1,128)} %bitcast.7), calls=%async_computation.1 | async-start | bytes 131072 | tf_op jit(solution)/shard_map/all_to_all | solution.py:20
  421.5 12.1 %collective-permute-start.1 = (f32[64]{0:T(128)S(1)}, f32[64]{0:T(128)S(1)}, u32[]{:S(2)}, u32[]{:S(2)}) collective-permute-start(f32[64]{0:T(128)S(1)} %fusion.10), channel_id=1, source_target_pairs={{0,1},{1,0},{2,3},{3,2},{4,5},{5,4},{6,7},{7,6},{8,9},{9,8},{10,11... | collective-permute-start | bytes 776 | tf_op jit(solution)/shard_map/ppermute | solution.py:34
  421.9 11.6 %collective-permute-start = (f32[64]{0:T(128)S(1)}, f32[64]{0:T(128)S(1)}, u32[]{:S(2)}, u32[]{:S(2)}) collective-permute-start(f32[64]{0:T(128)S(1)} %fusion.6), channel_id=1, source_target_pairs={{0,1},{1,0},{2,3},{3,2},{4,5},{5,4},{6,7},{7,6},{8,9},{9,8},{10,11... | collective-permute-start | bytes 776 | tf_op jit(solution)/shard_map/ppermute | solution.py:34
